TPU v7x, 32 devices: a whole 2x2x4 slice. The times are simulated.
32 devices in a mesh: dp: 4 (over x, core), fsdp: 8 (over z, y).
Axes of the slice: x: 2, y: 2, z: 4, core: 2. Of those that a mesh axis runs over, the one named last changes fastest.
Arguments:
- text_rows: bfloat16 [64, 512, 768], P(('dp', 'fsdp')), may hold values from -6 to 6
- visual_matrix: bfloat16 [768, 768], P('fsdp'), may hold values from -0.21875 to 0.21875
- batch_gain: bfloat16 [768], P('fsdp'), may hold values from 0.5 to 1.5
- batch_shift: bfloat16 [768], P('fsdp'), may hold values from -2.5 to 2.5
- attend_weight: bfloat16 [768, 2304], P('fsdp'), may hold values from -0.21875 to 0.21875
- merge_weight: bfloat16 [768, 768], P('fsdp'), may hold values from -1.75 to 1.75
- first_gain: bfloat16 [768], P('fsdp'), may hold values from 0.5 to 1.5
- first_shift: bfloat16 [768], P('fsdp'), may hold values from -2.5 to 2.5
- up_matrix: bfloat16 [768, 3072], P('fsdp'), may hold values from -0.21875 to 0.21875
- down_matrix: bfloat16 [3072, 768], P('fsdp'), may hold values from -0.109375 to 0.109375
- second_gain: bfloat16 [768], P('fsdp'), may hold values from 0.5 to 1.5
- second_shift: bfloat16 [768], P('fsdp'), may hold values from -2.5 to 2.5
- segment_counts: int32 [64], P(('dp', 'fsdp')), may hold values from 5 to 128, as said below
- segment_ids: int32 [64, 512], P(('dp', 'fsdp')), may hold values from -1 to 127, as said below
- padding_mask: int32 [64, 512], P(('dp', 'fsdp')), may hold values from 0 to 1, as said below
- cotangent: bfloat16 [64, 512, 768], P(('dp', 'fsdp')), may hold values from -6 to 6
Outputs:
- layer_output: float32 [64, 512, 768], P(('dp', 'fsdp'))
- text_gradient: float32 [64, 512, 768], P(('dp', 'fsdp'))
- visual_gradient: float32 [768, 768], P('fsdp')
- batch_gain_gradient: float32 [768], P('fsdp')
- batch_shift_gradient: float32 [768], P('fsdp')
- attend_gradient: float32 [768, 2304], P('fsdp')
- merge_gradient: float32 [768, 768], P('fsdp')
- first_gain_gradient: float32 [768], P('fsdp')
- first_shift_gradient: float32 [768], P('fsdp')
- up_gradient: float32 [768, 3072], P('fsdp')
- down_gradient: float32 [3072, 768], P('fsdp')
- second_gain_gradient: float32 [768], P('fsdp')
- second_shift_gradient: float32 [768], P('fsdp')
Inputs may be any that keep to these rules, and one draw needn't show every extreme that they name: On every device of dp+fsdp one of its documents has exactly 128 segments; segment_counts[d] is one more than the largest segment_ids in document d. `segment_ids`: A document's real rows come first and form segment_counts consecutive runs of one or more rows, numbered 0, 1, ... in order; padding rows hold -1. `padding_mask`: 1 exactly on the rows whose segment id is not -1, which are the first 256 or more rows of a document.
All inputs are finite; a program needn't handle non-finite values.
Results may differ from a plain program's by a relative error of at most 0.023.
The roundings to bfloat16 on the way count: a program that leaves them out, or rounds other values in their place, can miss the bound.
Values may be sent and summed in bfloat16 or wider, within the bound.
No kernel may reach another device: no remote copies, remote signals or barrier semaphores. Data moves between devices by JAX's collectives and lax.ppermute only.
A program may use at most 192 MiB of HBM per device.

v0:
```python
import jax
import jax.numpy as jnp
from jax import lax
from jax.sharding import PartitionSpec as P

HEADS = 12
SEGMAX = 128
eps_norm = 1e-05
eps_batch = 1e-05
masked_score = -1e30
highest_precision = lax.Precision.HIGHEST


def layer_norm(values, gain, shift):
    center = values - jnp.mean(values, axis=-1, keepdims=True)
    variance = jnp.mean(center * center, axis=-1, keepdims=True)
    return center * lax.rsqrt(variance + eps_norm) * gain + shift


def exact_gelu(values):
    return jax.nn.gelu(values, approximate=False)


def split_heads(packed):
    length = packed.shape[0]
    features = packed.shape[1] // 3
    head_size = features // HEADS
    queries = packed[:, :features].reshape(length, HEADS, head_size)
    keys_part = packed[:, features : 2 * features].reshape(length, HEADS, head_size)
    values_part = packed[:, 2 * features :].reshape(length, HEADS, head_size)
    return (queries, keys_part, values_part, head_size ** (-0.5))


def masked_scores(queries, keys_part, key_mask, scaling):
    scores = (
        jnp.einsum("qhe,khe->hqk", queries, keys_part, preferred_element_type=jnp.float32) * scaling
    )
    return jnp.where(key_mask[None, None, :] > 0, scores, masked_score)


def attend_doc(operands):
    packed, key_mask = operands
    queries, keys_part, values_part, scaling = split_heads(packed)
    scores = masked_scores(queries, keys_part, key_mask, scaling)
    top_score = jnp.max(scores, axis=-1, keepdims=True)
    unnormed = jnp.exp(scores - top_score)
    totals = jnp.sum(unnormed, axis=-1, keepdims=True)
    attention = unnormed / totals
    mixed = jnp.einsum(
        "hqk,khe->qhe",
        attention.astype(jnp.bfloat16),
        values_part,
        preferred_element_type=jnp.float32,
    )
    log_total = (top_score + jnp.log(totals))[..., 0]
    return (mixed.reshape(packed.shape[0], packed.shape[1] // 3).astype(jnp.bfloat16), log_total)


def attend_back(operands):
    packed, key_mask, log_total, delta_attended = operands
    queries, keys_part, values_part, scaling = split_heads(packed)
    length = packed.shape[0]
    features = packed.shape[1] // 3
    scores = masked_scores(queries, keys_part, key_mask, scaling)
    attention = jnp.exp(scores - log_total[..., None])
    delta_heads = delta_attended.reshape(length, HEADS, features // HEADS)
    delta_attention = jnp.einsum(
        "qhe,khe->hqk", delta_heads, values_part, preferred_element_type=jnp.float32
    )
    delta_scores = attention * (
        delta_attention - jnp.sum(attention * delta_attention, axis=-1, keepdims=True)
    )
    delta_low = delta_scores.astype(jnp.bfloat16)
    delta_queries = (
        jnp.einsum("hqk,khe->qhe", delta_low, keys_part, preferred_element_type=jnp.float32)
        * scaling
    )
    delta_keys = (
        jnp.einsum("hqk,qhe->khe", delta_low, queries, preferred_element_type=jnp.float32) * scaling
    )
    delta_values = jnp.einsum(
        "hqk,qhe->khe",
        attention.astype(jnp.bfloat16),
        delta_heads,
        preferred_element_type=jnp.float32,
    )
    merged = jnp.concatenate(
        [
            delta_queries.reshape(length, features),
            delta_keys.reshape(length, features),
            delta_values.reshape(length, features),
        ],
        axis=1,
    )
    return merged.astype(jnp.bfloat16)


def shards(
    text_rows,
    visual_matrix,
    batch_gain,
    batch_shift,
    attend_weight,
    merge_weight,
    first_gain,
    first_shift,
    up_matrix,
    down_matrix,
    second_gain,
    second_shift,
    segment_counts,
    segment_ids,
    padding_mask,
    cotangent,
):
    gathered = (
        lax.all_gather(visual_matrix, "fsdp", axis=0, tiled=True),
        lax.all_gather(batch_gain, "fsdp", axis=0, tiled=True),
        lax.all_gather(batch_shift, "fsdp", axis=0, tiled=True),
        lax.all_gather(attend_weight, "fsdp", axis=0, tiled=True),
        lax.all_gather(merge_weight, "fsdp", axis=0, tiled=True),
        lax.all_gather(first_gain, "fsdp", axis=0, tiled=True),
        lax.all_gather(first_shift, "fsdp", axis=0, tiled=True),
        lax.all_gather(up_matrix, "fsdp", axis=0, tiled=True),
        lax.all_gather(down_matrix, "fsdp", axis=0, tiled=True),
        lax.all_gather(second_gain, "fsdp", axis=0, tiled=True),
        lax.all_gather(second_shift, "fsdp", axis=0, tiled=True),
    )
    (
        gathered_visual_weight,
        full_batch_gain,
        full_batch_shift,
        full_attend,
        full_merge,
        full_first_gain,
        full_first_shift,
        gathered_up_weight,
        gathered_down_weight,
        full_second_gain,
        full_second_shift,
    ) = gathered
    features = text_rows.shape[2]
    slot_index = jnp.arange(SEGMAX)
    matches = segment_ids[:, :, None] == slot_index[None, None, :]
    onehot = matches.astype(jnp.bfloat16)
    onehot_wide = matches.astype(jnp.float32)
    divisor = jnp.maximum(jnp.sum(onehot_wide, axis=1), 1.0)[..., None]
    pooled_segments = (
        jnp.einsum("drs,drc->dsc", onehot, text_rows, preferred_element_type=jnp.float32) / divisor
    ).astype(jnp.bfloat16)
    visual_rows = jnp.einsum(
        "bil,ly->biy", pooled_segments, gathered_visual_weight, preferred_element_type=jnp.float32
    )
    valid_slot = (slot_index[None, :] < segment_counts[:, None]).astype(jnp.float32)[..., None]
    local_count = jnp.sum(segment_counts).astype(jnp.float32)
    masked_visual = valid_slot * visual_rows
    segment_total, visual_sum = lax.psum(
        (local_count, jnp.sum(masked_visual, axis=(0, 1))), ("dp", "fsdp")
    )
    batch_center = visual_sum / segment_total
    center = visual_rows - batch_center
    variance = (
        lax.psum(jnp.sum(valid_slot * center * center, axis=(0, 1)), ("dp", "fsdp")) / segment_total
    )
    inverse_spread = lax.rsqrt(variance + eps_batch)
    normed = center * inverse_spread
    embedded = (
        normed * full_batch_gain.astype(jnp.float32) + full_batch_shift.astype(jnp.float32)
    ).astype(jnp.bfloat16)
    joined = text_rows.astype(jnp.float32) + jnp.einsum(
        "drs,dsc->drc", onehot, embedded, preferred_element_type=jnp.float32
    )
    joined_low = joined.astype(jnp.bfloat16)
    packed = jnp.einsum(
        "drc,ce->dre", joined_low, full_attend, preferred_element_type=jnp.float32
    ).astype(jnp.bfloat16)
    attended, log_total = lax.map(attend_doc, (packed, padding_mask))
    projected = jnp.einsum("drc,ce->dre", attended, full_merge, preferred_element_type=jnp.float32)
    pre_one = joined + projected
    hidden_state = layer_norm(
        pre_one, full_first_gain.astype(jnp.float32), full_first_shift.astype(jnp.float32)
    )
    hidden_reduced_precision = hidden_state.astype(jnp.bfloat16)
    inner_hidden = jnp.einsum(
        "sjq,qy->sjy",
        hidden_reduced_precision,
        gathered_up_weight,
        preferred_element_type=jnp.float32,
    )
    gelu_activated = exact_gelu(inner_hidden).astype(jnp.bfloat16)
    residual_branch = jnp.einsum(
        "zya,av->zyv", gelu_activated, gathered_down_weight, preferred_element_type=jnp.float32
    )
    pre_two = hidden_state + residual_branch
    layer_output = layer_norm(
        pre_two, full_second_gain.astype(jnp.float32), full_second_shift.astype(jnp.float32)
    )
    again = (
        lax.all_gather(visual_matrix, "fsdp", axis=0, tiled=True),
        lax.all_gather(batch_gain, "fsdp", axis=0, tiled=True),
        lax.all_gather(attend_weight, "fsdp", axis=0, tiled=True),
        lax.all_gather(merge_weight, "fsdp", axis=0, tiled=True),
        lax.all_gather(first_gain, "fsdp", axis=0, tiled=True),
        lax.all_gather(up_matrix, "fsdp", axis=0, tiled=True),
        lax.all_gather(down_matrix, "fsdp", axis=0, tiled=True),
        lax.all_gather(second_gain, "fsdp", axis=0, tiled=True),
    )
    (
        visual_pullback,
        back_batch_gain,
        back_attend,
        back_merge,
        back_first_gain,
        up_pullback,
        down_pullback,
        back_second_gain,
    ) = again
    second_back = jax.vjp(
        layer_norm,
        pre_two,
        back_second_gain.astype(jnp.float32),
        full_second_shift.astype(jnp.float32),
    )[1]
    delta_two, second_gain_local, second_shift_local = second_back(cotangent.astype(jnp.float32))
    branch_gradient = delta_two.astype(jnp.bfloat16)
    down_local = jnp.einsum(
        "omt,oms->ts", gelu_activated, branch_gradient, preferred_element_type=jnp.float32
    )
    delta_activated = jnp.einsum(
        "ivj,hj->ivh", branch_gradient, down_pullback, preferred_element_type=jnp.float32
    )
    gelu_back = jax.vjp(exact_gelu, inner_hidden)[1]
    inner_gradient = gelu_back(delta_activated)[0].astype(jnp.bfloat16)
    up_local = jnp.einsum(
        "oih,oiu->hu", hidden_reduced_precision, inner_gradient, preferred_element_type=jnp.float32
    )
    delta_hidden = delta_two + jnp.einsum(
        "wmx,ix->wmi", inner_gradient, up_pullback, preferred_element_type=jnp.float32
    )
    first_back = jax.vjp(
        layer_norm,
        pre_one,
        back_first_gain.astype(jnp.float32),
        full_first_shift.astype(jnp.float32),
    )[1]
    delta_one, first_gain_local, first_shift_local = first_back(delta_hidden)
    delta_projected = delta_one.astype(jnp.bfloat16)
    merge_local = jnp.einsum(
        "drc,dre->ce", attended, delta_projected, preferred_element_type=jnp.float32
    )
    delta_attended = jnp.einsum(
        "dre,ce->drc", delta_projected, back_merge, preferred_element_type=jnp.float32
    ).astype(jnp.bfloat16)
    delta_packed = lax.map(attend_back, (packed, padding_mask, log_total, delta_attended))
    attend_local = jnp.einsum(
        "drc,dre->ce", joined_low, delta_packed, preferred_element_type=jnp.float32
    )
    delta_joined = delta_one + jnp.einsum(
        "dre,ce->drc", delta_packed, back_attend, preferred_element_type=jnp.float32
    )
    delta_embedded = jnp.einsum(
        "drs,drc->dsc",
        onehot_wide,
        delta_joined,
        precision=highest_precision,
        preferred_element_type=jnp.float32,
    )
    shift_total, gain_total = lax.psum(
        (jnp.sum(delta_embedded, axis=(0, 1)), jnp.sum(delta_embedded * normed, axis=(0, 1))),
        ("dp", "fsdp"),
    )
    visual_delta_rows = (
        valid_slot
        * back_batch_gain.astype(jnp.float32)
        * inverse_spread
        * (delta_embedded - shift_total / segment_total - normed * gain_total / segment_total)
    ).astype(jnp.bfloat16)
    visual_local = jnp.einsum(
        "bli,blz->iz", pooled_segments, visual_delta_rows, preferred_element_type=jnp.float32
    )
    delta_pooled = (
        jnp.einsum(
            "zbl,wl->zbw", visual_delta_rows, visual_pullback, preferred_element_type=jnp.float32
        )
        / divisor
    )
    text_gradient = delta_joined + jnp.einsum(
        "drs,dsc->drc",
        onehot_wide,
        delta_pooled,
        precision=highest_precision,
        preferred_element_type=jnp.float32,
    )
    (
        visual_shard,
        attend_shard,
        merge_shard,
        first_gain_shard,
        first_shift_shard,
        up_shard,
        down_shard,
        second_gain_shard,
        second_shift_shard,
    ) = (
        lax.psum_scatter(
            visual_local.astype(jnp.bfloat16), "fsdp", scatter_dimension=0, tiled=True
        ).astype(jnp.float32),
        lax.psum_scatter(
            attend_local.astype(jnp.bfloat16), "fsdp", scatter_dimension=0, tiled=True
        ).astype(jnp.float32),
        lax.psum_scatter(
            merge_local.astype(jnp.bfloat16), "fsdp", scatter_dimension=0, tiled=True
        ).astype(jnp.float32),
        lax.psum_scatter(
            first_gain_local.astype(jnp.bfloat16), "fsdp", scatter_dimension=0, tiled=True
        ).astype(jnp.float32),
        lax.psum_scatter(
            first_shift_local.astype(jnp.bfloat16), "fsdp", scatter_dimension=0, tiled=True
        ).astype(jnp.float32),
        lax.psum_scatter(
            up_local.astype(jnp.bfloat16), "fsdp", scatter_dimension=0, tiled=True
        ).astype(jnp.float32),
        lax.psum_scatter(
            down_local.astype(jnp.bfloat16), "fsdp", scatter_dimension=0, tiled=True
        ).astype(jnp.float32),
        lax.psum_scatter(
            second_gain_local.astype(jnp.bfloat16), "fsdp", scatter_dimension=0, tiled=True
        ).astype(jnp.float32),
        lax.psum_scatter(
            second_shift_local.astype(jnp.bfloat16), "fsdp", scatter_dimension=0, tiled=True
        ).astype(jnp.float32),
    )
    summed = (
        lax.psum(visual_shard.astype(jnp.bfloat16), "dp").astype(jnp.float32),
        lax.psum(attend_shard.astype(jnp.bfloat16), "dp").astype(jnp.float32),
        lax.psum(merge_shard.astype(jnp.bfloat16), "dp").astype(jnp.float32),
        lax.psum(first_gain_shard.astype(jnp.bfloat16), "dp").astype(jnp.float32),
        lax.psum(first_shift_shard.astype(jnp.bfloat16), "dp").astype(jnp.float32),
        lax.psum(up_shard.astype(jnp.bfloat16), "dp").astype(jnp.float32),
        lax.psum(down_shard.astype(jnp.bfloat16), "dp").astype(jnp.float32),
        lax.psum(second_gain_shard.astype(jnp.bfloat16), "dp").astype(jnp.float32),
        lax.psum(second_shift_shard.astype(jnp.bfloat16), "dp").astype(jnp.float32),
    )
    (
        visual_gradient,
        attend_gradient,
        merge_gradient,
        first_gain_gradient,
        first_shift_gradient,
        up_gradient,
        down_gradient,
        second_gain_gradient,
        second_shift_gradient,
    ) = summed
    piece = features // lax.axis_size("fsdp")
    start = lax.axis_index("fsdp") * piece
    batch_gain_gradient = lax.dynamic_slice_in_dim(gain_total, start, piece, 0)
    batch_shift_gradient = lax.dynamic_slice_in_dim(shift_total, start, piece, 0)
    return (
        layer_output,
        text_gradient,
        visual_gradient,
        batch_gain_gradient,
        batch_shift_gradient,
        attend_gradient,
        merge_gradient,
        first_gain_gradient,
        first_shift_gradient,
        up_gradient,
        down_gradient,
        second_gain_gradient,
        second_shift_gradient,
    )


def solution(mesh):
    in_specs = (
        P(("dp", "fsdp"), None, None),
        P("fsdp", None),
        P("fsdp"),
        P("fsdp"),
        P("fsdp", None),
        P("fsdp", None),
        P("fsdp"),
        P("fsdp"),
        P("fsdp", None),
        P("fsdp", None),
        P("fsdp"),
        P("fsdp"),
        P(("dp", "fsdp")),
        P(("dp", "fsdp"), None),
        P(("dp", "fsdp"), None),
        P(("dp", "fsdp"), None, None),
    )
    out_specs = (
        P(("dp", "fsdp"), None, None),
        P(("dp", "fsdp"), None, None),
        P("fsdp", None),
        P("fsdp"),
        P("fsdp"),
        P("fsdp", None),
        P("fsdp", None),
        P("fsdp"),
        P("fsdp"),
        P("fsdp", None),
        P("fsdp", None),
        P("fsdp"),
        P("fsdp"),
    )
    return jax.shard_map(shards, mesh=mesh, in_specs=in_specs, out_specs=out_specs, check_vma=False)
```

profile of v0, /device:TPU:0, one launch (start us, length us, event | category | flops | bytes accessed | tf_op | source)
XLA Modules:
  0.0 913.8 jit_solution(14838720792702939342)
XLA Ops:
  20.4 39.1 %all-reduce.13 = (bf16[768]{0:T(1024)(128)(2,1)S(1)}, bf16[768]{0:T(1024)(128)(2,1)S(1)}, bf16[768]{0:T(1024)(128)(2,1)S(1)}, bf16[768]{0:T(1024)(128)(2,1)S(1)}, bf16[768]{0:T(1024)(128)(2,1)S(1)}) all-reduce(bf16[768]{0:T(1024)(128)(2,1)S(1)} %dynamic-update-slice.1, ...), channel_id=1, replica_groups=mesh['dp'=4,'fsdp'=8] {'fsdp'}, use_global_device_ids=true, to_apply=%add.1 | all-reduce | flops 3840 | bytes 15360
  61.3 2.1 fusion.47
  63.5 2.0 multiply_reduce_fusion.6
  65.5 38.1 %all-reduce.11 = (f32[768]{0:T(1024)S(1)}, f32[]{:T(128)}) all-reduce(f32[768]{0:T(1024)S(1)} %get-tuple-element.172, f32[]{:T(128)S(6)} %convert_element_type.181), channel_id=1, replica_groups=mesh['dp'=4,'fsdp'=8] {'dp','fsdp'}, use_global_device_ids=true, to_apply=%region_2.0 | all-reduce | flops 769 | bytes 6152 | tf_op jit(solution)/shard_map/psum | solution.py:157
  104.5 42.7 %psum.100 = f32[768]{0:T(1024)S(1)} all-reduce(f32[768]{0:T(1024)S(1)} %fusion.53), channel_id=1, replica_groups=mesh['dp'=4,'fsdp'=8] {'dp','fsdp'}, use_global_device_ids=true, to_apply=%region_6.0 | all-reduce | flops 768 | bytes 6144 | tf_op jit(solution)/shard_map/psum | solution.py:163
  147.8 2.3 fusion.55
  150.1 9.0 convolution_convert_fusion
  159.1 6.8 copy.50
  165.9 22.8 %while.22 = (s32[]{:T(128)}, bf16[2,512,768]{1,2,0:T(8,128)(2,1)S(1)}, f32[2,12,512]{2,1,0:T(8,128)S(1)}, bf16[2,512,2304]{1,2,0:T(8,128)(2,1)}, s32[2,512]{1,0:T(2,128)S(1)}, /*index=5*/s32[]{:T(128)}) while((s32[]{:T(128)}, bf16[2,512,768]{1,2,0:T(8,128)(2,1)S(1)}, f32[2,12,512]{2,1,0:T(8,128)S(1)}, bf16[2,512,2304]{1,2,0:T(8,128)(2,1)}, ...), condition=%wide.region_10.11_spmd, body=%wide.region_7.10_spmd.sunk | while | flops 843442688 | bytes 52129876 | solution.py:177
  166.4 1.8 dynamic-slice_bitcast_fusion.6
  168.4 3.1 fusion.131
  171.5 2.6 fusion.132
  174.1 3.3 fusion.133
  177.5 1.8 dynamic-slice_bitcast_fusion.6
  179.5 3.1 fusion.131
  182.6 2.6 fusion.132
  185.2 3.3 fusion.133
  189.9 4.8 fusion.77
  195.2 48.8 %all-gather.12.cloned.1.call-done = bf16[768,3072]{1,0:T(8,128)(2,1)} async-done(((bf16[96,3072]{1,0:T(8,128)(2,1)}), bf16[768,3072]{1,0:T(8,128)(2,1)}) %all-gather.12.cloned.1.call-update) | async-done | bytes 4718608 | tf_op jit(solution)/shard_map/all_gather | solution.py:124
  244.0 14.9 %fusion.36 = (u8[512,3072]{1,0:T(8,128)(4,1)S(1)}, u8[512,3072]{1,0:T(8,128)(4,1)S(1)}, f32[2,512,3072]{2,1,0:T(8,128)}) fusion(bf16[768,3072]{1,0:T(8,128)(2,1)} %all-gather.12.cloned.1.call-done, f32[2,512,768]{2,1,0:T(8,128)S(1)} %get-tuple-element.175, f32[768]{0:T(1024)S(1)} %copy-done.50, f32[768]{0:T(1024)S(1)} %copy-done.40, ...), kind=kOutput, calls=%fused_computation.80 | convolution fusion | flops 4873519104 | bytes 23607296 | tf_op jit(solution)/shard_map/sjq,qy->sjy/dot_general | solution.py:184
  258.9 31.0 %multiply_convert_fusion.3 = (bf16[2,512,3072]{2,1,0:T(8,128)(2,1)}, f32[2,512,3072]{2,1,0:T(8,128)}) fusion(f32[2,512,3072]{2,1,0:T(8,128)} %get-tuple-element.176, u8[512,3072]{1,0:T(8,128)(4,1)S(1)} %get-tuple-element.99, u8[512,3072]{1,0:T(8,128)(4,1)S(1)} %get-tuple-element.98), kind=kLoop, calls=%fused_computation.37 | loop fusion | flops 220200960 | bytes 34603008 | tf_op jit(solution)/shard_map/convert_element_type | solution.py:190
  289.9 34.1 %all-gather.14.cloned.1.call-done = bf16[3072,768]{1,0:T(8,128)(2,1)} async-done(((bf16[384,768]{1,0:T(8,128)(2,1)}), bf16[3072,768]{1,0:T(8,128)(2,1)}) %all-gather.14.cloned.1.call-update) | async-done | bytes 4718608 | tf_op jit(solution)/shard_map/all_gather | solution.py:125
  324.1 9.5 %fusion.78 = (f32[2,512]{1,0:T(2,128)S(1)}, f32[2,512,768]{2,1,0:T(8,128)S(1)}) fusion(bf16[2,512,3072]{2,1,0:T(8,128)(2,1)} %get-tuple-element.156, bf16[3072,768]{1,0:T(8,128)(2,1)} %all-gather.14.cloned.1.call-done, f32[768]{0:T(1024)S(1)} %copy-done.50, f32[768]{0:T(1024)S(1)} %copy-done.40, f32[2,512]{1,0:T(2,128)S(1)} %fusion.66, ...), kind=kOutput, calls=%fused_computation.142 | convolution fusion | flops 4836555776 | bytes 17319936 | tf_op jit(solution)/shard_map/zya,av->zyv/dot_general | solution.py:191
  334.7 2.4 fusion.34
  337.1 16.4 %add_convert_fusion = bf16[2,512,3072]{2,1,0:T(8,128)(2,1)} fusion(f32[2,512,3072]{2,1,0:T(8,128)} %get-tuple-element.157, f32[2,512,3072]{2,1,0:T(8,128)} %get-tuple-element.176, bf16[3072,768]{1,0:T(8,128)(2,1)} %all-gather.14.cloned.1.call-done, f32[2,512]{1,0:T(2,128)S(1)} %negate_multiply_fusion.2, bf16[2,512,768]{2,1,0:T(8,128)(2,1)} %param.35, ...), kind=kOutput, calls=%fused_computation.36 | convolution fusion | flops 4882956288 | bytes 40913920 | tf_op jit(solution)/shard_map/ivj,hj->ivh/dot_general | solution.py:229
  353.5 11.2 %multiply_reduce_fusion.1 = (bf16[768]{0:T(1024)(128)(2,1)}, f32[2,512]{1,0:T(2,128)S(1)}, bf16[768]{0:T(1024)(128)(2,1)}, f32[2,512,768]{2,1,0:T(8,128)S(1)}) fusion(f32[2,512,768]{2,1,0:T(8,128)} %copy-done.2, f32[2,512]{1,0:T(2,128)S(1)} %fusion.66, f32[2,512]{1,0:T(2,128)S(1)} %broadcast_multiply_fusion.1, f32[768]{0:T(1024)S(1)} %copy-done.40, ...), kind=kOutput, calls=%fused_computation.72 | convolution fusion | flops 4845204480 | bytes 22057984 | tf_op jit(solution)/shard_map/wmx,ix->wmi/dot_general | solution.py:237
  366.1 2.5 bitcast_convert_fusion.3
  368.8 3.9 convolution_convert_fusion.1
  372.6 77.6 %while.23 = (s32[]{:T(128)}, bf16[2,512,2304]{1,2,0:T(8,128)(2,1)}, bf16[2,512,2304]{1,2,0:T(8,128)(2,1)}, s32[2,512]{1,0:T(2,128)S(1)}, f32[2,12,512]{2,1,0:T(8...) while((s32[]{:T(128)}, bf16[2,512,2304]{1,2,0:T(8,128)(2,1)}, bf16[2,512,2304]{1,2,0:T(8,128)(2,1)}, ...), condition=%wide.region_21.22_spmd, body=%wide.region_19.21_spmd.sunk | while | flops 2069490176 | bytes 163754704 | solution.py:254
  373.0 1.9 dynamic-slice_bitcast_fusion.7
  375.1 6.4 fusion.145
  383.9 11.5 %multiply_reduce_fusion.8 = (f32[12,512]{1,0:T(8,128)S(1)}, f32[12,512,512]{1,2,0:T(8,128)}) fusion(f32[12,512,512]{1,2,0:T(8,128)} %fusion.145, f32[12,512]{1,0:T(8,128)S(1)} %dynamic-slice_bitcast_fusion.8, pred[512]{0:T(512)(128)(4,1)S(1)} %compare_reduce_fusion.5, bf16[512,12,64]{0,2,1:T(8,128)(2,1)S(1)} %bitcast.169, ...), kind=kOutput, calls=%fused_computation.14.clone.1 | convolution fusion | flops 418375680 | bytes 26788352 | tf_op jit(solution)/shard_map/while/body/eval_jaxpr/qhe,khe->hqk/dot_general | solution.py:67
  396.7 7.1 multiply_convert_fusion.8
  405.0 2.0 multiply_convert_fusion.9
  407.0 3.1 fusion.146
  410.0 1.6 maximum_dynamic-update-slice_fusion.2
  411.6 1.8 dynamic-slice_bitcast_fusion.7
  413.6 6.4 fusion.145
  422.4 11.5 %multiply_reduce_fusion.8 = (f32[12,512]{1,0:T(8,128)S(1)}, f32[12,512,512]{1,2,0:T(8,128)}) fusion(f32[12,512,512]{1,2,0:T(8,128)} %fusion.145, f32[12,512]{1,0:T(8,128)S(1)} %dynamic-slice_bitcast_fusion.8, pred[512]{0:T(512)(128)(4,1)S(1)} %compare_reduce_fusion.5, bf16[512,12,64]{0,2,1:T(8,128)(2,1)S(1)} %bitcast.169, ...), kind=kOutput, calls=%fused_computation.14.clone.1 | convolution fusion | flops 418375680 | bytes 26788352 | tf_op jit(solution)/shard_map/while/body/eval_jaxpr/qhe,khe->hqk/dot_general | solution.py:67
  435.1 7.1 multiply_convert_fusion.8
  443.3 2.0 multiply_convert_fusion.9
  445.3 3.1 fusion.146
  448.4 1.6 maximum_dynamic-update-slice_fusion.2
  450.3 8.5 add_add_fusion.2
  458.8 1.6 copy-done.8
  460.4 1.5 fusion.71
  461.9 38.4 %all-reduce.10 = (f32[768]{0:T(1024)S(1)}, f32[768]{0:T(1024)S(1)}) all-reduce(f32[768]{0:T(1024)S(1)} %get-tuple-element.108, f32[768]{0:T(1024)S(1)} %get-tuple-element.107), channel_id=1, replica_groups=mesh['dp'=4,'fsdp'=8] {'dp','fsdp'}, use_global_device_ids=true, to_apply=%region_25.26 | all-reduce | flops 1536 | bytes 12288 | tf_op jit(solution)/shard_map/psum | solution.py:268
  502.7 1.5 bitcast_convert_fusion.4
  505.0 8.5 bitcast_convert_fusion.2
  513.8 1.6 copy-done.1
  515.4 11.2 %bitcast_convert_fusion = bf16[3072,768]{1,0:T(8,128)(2,1)} fusion(bf16[2,512,3072]{2,1,0:T(8,128)(2,1)} %get-tuple-element.156, f32[2,512]{1,0:T(2,128)S(1)} %copy-done.53, bf16[2,512,768]{2,1,0:T(8,128)(2,1)} %param.35, f32[2,512,768]{2,1,0:T(8,128)S(1)} %copy-done.1, f32[2,512]{1,0:T(2,128)S(1)} %copy-done.46, f32[768]{0:T(1024)S(1)} %copy-done.27, ...), kind=kOutput, calls=%fused_computation.50 | convolution fusion | flops 4841275392 | bytes 15748096 | tf_op jit(solution)/shard_map/omt,oms->ts/dot_general | solution.py:226
  527.3 10.5 %bitcast_convert_fusion.1 = bf16[768,3072]{1,0:T(8,128)(2,1)} fusion(bf16[2,512,3072]{2,1,0:T(8,128)(2,1)} %add_convert_fusion, f32[2,512,768]{2,1,0:T(8,128)} %copy-done.2, f32[768]{0:T(1024)S(1)} %copy-done.51, f32[768]{0:T(1024)S(1)} %copy-done.41, f32[2,512]{1,0:T(2,128)S(1)} %copy-done.43, f32[2,512]{1,0:T(2,128)S(1)} %copy-done.37), kind=kOutput, calls=%fused_computation.51 | convolution fusion | flops 4838129664 | bytes 14170112 | tf_op jit(solution)/shard_map/oih,oiu->hu/dot_general | solution.py:234
  537.9 2.3 reduce_sum.212
  545.3 37.0 %all-reduce.12 = (bf16[768]{0:T(1024)(128)(2,1)}, bf16[768]{0:T(1024)(128)(2,1)}, bf16[768]{0:T(1024)(128)(2,1)}, bf16[768]{0:T(1024)(128)(2,1)}, bf16[768]{0:T(1024)(128)(2,1)}) all-reduce(bf16[768]{0:T(1024)(128)(2,1)} %dynamic-update-slice.5, bf16[768]{0:T(1024)(128)(2,1)} %get-tuple-element.100, ...), channel_id=1, replica_groups=mesh['dp'=4,'fsdp'=8] {'fsdp'}, use_global_device_ids=true, to_apply=%add.5 | all-reduce | flops 3840 | bytes 15360
  587.4 6.9 all-reduce.14
  600.3 50.8 %reduce-scatter.8.cloned.1.call-done = bf16[96,2304]{1,0:T(8,128)(2,1)} async-done(((bf16[768,2304]{1,0:T(8,128)(2,1)}), bf16[96,2304]{1,0:T(8,128)(2,1)}) %reduce-scatter.8.cloned.1.call-update) | async-done | bytes 442384 | tf_op jit(solution)/shard_map/reduce_scatter | solution.py:308
  651.0 98.7 %reduce-scatter.14.cloned.1.call-done = bf16[384,768]{1,0:T(8,128)(2,1)} async-done(((bf16[3072,768]{1,0:T(8,128)(2,1)}), bf16[384,768]{1,0:T(8,128)(2,1)}) %reduce-scatter.14.cloned.1.call-update) | async-done | bytes 589840 | tf_op jit(solution)/shard_map/reduce_scatter | solution.py:323
  749.7 98.5 %reduce-scatter.12.cloned.1.call-done = bf16[96,3072]{1,0:T(8,128)(2,1)} async-done(((bf16[768,3072]{1,0:T(8,128)(2,1)}), bf16[96,3072]{1,0:T(8,128)(2,1)}) %reduce-scatter.12.cloned.1.call-update) | async-done | bytes 589840 | tf_op jit(solution)/shard_map/reduce_scatter | solution.py:320
  848.3 1.8 convolution_divide_fusion
  850.1 2.2 multiply_add_fusion
  853.0 3.2 convolution_add_fusion
  856.2 44.0 %all-reduce.18.cloned.1.call-done = (bf16[96,768]{1,0:T(8,128)(2,1)}, bf16[96,2304]{1,0:T(8,128)(2,1)}, bf16[96,768]{1,0:T(8,128)(2,1)}, bf16[96,3072]{1,0:T(8,128)(2,1)}, bf16[384,768]{1,0:T(8,128)(2,1)}) async-done(((bf16[96,768]{1,0:T(8,128)(2,1)}, bf16[96,2304]{1,0:T(8,128)(2,1)}, bf16[96,768]{1,0:T(8,128)(2,1)}, bf16[96,3072]{1,0:T(8,128)(2,1)}, bf16[384,768]{1,0:T(8,128)(2,1)}), ...) | async-done | bytes 1916944 | tf_op jit(solution)/shard_map/psum | solution.py:334
  900.2 2.2 convert_element_type.210
  902.4 2.2 convert_element_type.212
  (231 shorter events, 52.4 us)
Async XLA Ops:
  7.2 56.3 %all-gather.6.cloned.1.call-start = ((), (), s32[]{:S(2)}) async-start(), calls=%async_computation.5 | async-start | bytes 1327104 | tf_op jit(solution)/shard_map/all_gather | solution.py:117
  7.9 142.2 %all-gather.8.cloned.1.call-start = ((), (), s32[]{:S(2)}) async-start(), calls=%async_computation.6 | async-start | bytes 3981312 | tf_op jit(solution)/shard_map/all_gather | solution.py:120
  8.7 180.1 %all-gather.10.cloned.1.call-start = ((), (), s32[]{:S(2)}) async-start(), calls=%async_computation.7 | async-start | bytes 1327104 | tf_op jit(solution)/shard_map/all_gather | solution.py:121
  9.4 234.6 %all-gather.12.cloned.1.call-start = ((), (), s32[]{:S(2)}) async-start(), calls=%async_computation.8 | async-start | bytes 5308416 | tf_op jit(solution)/shard_map/all_gather | solution.py:124
  10.0 314.1 %all-gather.14.cloned.1.call-start = ((), (), s32[]{:S(2)}) async-start(), calls=%async_computation.9 | async-start | bytes 5308416 | tf_op jit(solution)/shard_map/all_gather | solution.py:125
  10.6 589.7 %reduce-scatter.10.cloned.1.call-start = ((), (), s32[]{:S(2)}) async-start(), calls=%async_computation.12 | async-start | bytes 1327104 | tf_op jit(solution)/shard_map/reduce_scatter | solution.py:311
  11.4 92.9 %copy-start.47 = (f32[2,128]{1,0:T(2,128)}, f32[2,128]{1,0:T(2,128)S(1)}, u32[]{:S(2)}) copy-start(f32[2,128]{1,0:T(2,128)S(1)} %compare_convert_fusion) | copy-start | bytes 3076
  13.6 49.9 %copy-start.57 = (f32[2,128]{1,0:T(2,128)}, f32[2,128]{1,0:T(2,128)S(1)}, u32[]{:S(2)}) copy-start(f32[2,128]{1,0:T(2,128)S(1)} %broadcast_maximum_fusion) | copy-start | bytes 3076
  59.5 88.3 %copy-start.34 = (f32[768]{0:T(1024)}, f32[768]{0:T(1024)S(1)}, u32[]{:S(2)}) copy-start(f32[768]{0:T(1024)S(1)} %convert_element_type.182) | copy-start | bytes 9220
  61.3 86.5 %copy-start.30 = (s32[2,512]{1,0:T(2,128)S(1)}, s32[2,512]{1,0:T(2,128)}, u32[]{:S(2)}) copy-start(s32[2,512]{1,0:T(2,128)} %param.33) | copy-start | bytes 12292
  63.4 86.7 %copy-start.16 = (bf16[2,128,768]{2,1,0:T(8,128)(2,1)}, bf16[2,128,768]{2,1,0:T(8,128)(2,1)S(1)}, u32[]{:S(2)}) copy-start(bf16[2,128,768]{2,1,0:T(8,128)(2,1)S(1)} %fusion.47) | copy-start | bytes 1179652
  63.5 86.7 %copy-start.12 = (bf16[2,512,768]{2,1,0:T(8,128)(2,1)S(1)}, bf16[2,512,768]{2,1,0:T(8,128)(2,1)}, u32[]{:S(2)}) copy-start(bf16[2,512,768]{2,1,0:T(8,128)(2,1)} %param.20) | copy-start | bytes 4718596
  65.5 93.5 %copy-start.4 = (f32[2,128,768]{2,1,0:T(8,128)}, f32[2,128,768]{2,1,0:T(8,128)S(1)}, u32[]{:S(2)}) copy-start(f32[2,128,768]{2,1,0:T(8,128)S(1)} %get-tuple-element.173) | copy-start | bytes 2359300
  104.3 54.8 %copy-start.24 = (f32[768]{0:T(1024)}, f32[768]{0:T(1024)S(1)}, u32[]{:S(2)}) copy-start(f32[768]{0:T(1024)S(1)} %broadcast_divide_fusion.1) | copy-start | bytes 9220
  147.8 11.3 %copy-start.32 = (f32[768]{0:T(1024)}, f32[768]{0:T(1024)S(1)}, u32[]{:S(2)}) copy-start(f32[768]{0:T(1024)S(1)} %add_rsqrt_fusion) | copy-start | bytes 9220
  159.1 6.8 copy-start.13
  159.1 6.8 copy-start.23
  194.6 64.2 %copy-start.2 = (f32[2,512,768]{2,1,0:T(8,128)}, f32[2,512,768]{2,1,0:T(8,128)S(1)}, u32[]{:S(2)}) copy-start(f32[2,512,768]{2,1,0:T(8,128)S(1)} %get-tuple-element.175) | copy-start | bytes 9437188
  194.6 49.3 %copy-start.40 = (f32[768]{0:T(1024)S(1)}, f32[768]{0:T(1024)}, u32[]{:S(2)}) copy-start(f32[768]{0:T(1024)} %convert_element_type.187) | copy-start | bytes 9220
  194.7 49.3 %copy-start.50 = (f32[768]{0:T(1024)S(1)}, f32[768]{0:T(1024)}, u32[]{:S(2)}) copy-start(f32[768]{0:T(1024)} %convert_element_type.188) | copy-start | bytes 9220
  194.7 170.0 %copy-start.36 = (f32[2,512]{1,0:T(2,128)}, f32[2,512]{1,0:T(2,128)S(1)}, u32[]{:S(2)}) copy-start(f32[2,512]{1,0:T(2,128)S(1)} %broadcast_multiply_fusion.1) | copy-start | bytes 12292
  195.2 169.5 %copy-start.42 = (f32[2,512]{1,0:T(2,128)}, f32[2,512]{1,0:T(2,128)S(1)}, u32[]{:S(2)}) copy-start(f32[2,512]{1,0:T(2,128)S(1)} %fusion.66) | copy-start | bytes 12292
  324.1 9.6 %copy-start.6 = (bf16[2,512,768]{2,1,0:T(8,128)(2,1)S(1)}, bf16[2,512,768]{2,1,0:T(8,128)(2,1)}, u32[]{:S(2)}) copy-start(bf16[2,512,768]{2,1,0:T(8,128)(2,1)} %param.35) | copy-start | bytes 4718596
  324.1 9.6 %copy-start.26 = (f32[768]{0:T(1024)S(1)}, f32[768]{0:T(1024)}, u32[]{:S(2)}) copy-start(f32[768]{0:T(1024)} %convert_element_type.191) | copy-start | bytes 9220
  333.6 19.8 %copy-start = (f32[2,512,768]{2,1,0:T(8,128)}, f32[2,512,768]{2,1,0:T(8,128)S(1)}, u32[]{:S(2)}) copy-start(f32[2,512,768]{2,1,0:T(8,128)S(1)} %get-tuple-element.178) | copy-start | bytes 9437188
  333.6 19.8 %copy-start.28 = (f32[2,512]{1,0:T(2,128)}, f32[2,512]{1,0:T(2,128)S(1)}, u32[]{:S(2)}) copy-start(f32[2,512]{1,0:T(2,128)S(1)} %broadcast_multiply_fusion) | copy-start | bytes 12292
  334.7 18.8 %copy-start.38 = (f32[2,512]{1,0:T(2,128)}, f32[2,512]{1,0:T(2,128)S(1)}, u32[]{:S(2)}) copy-start(f32[2,512]{1,0:T(2,128)S(1)} %get-tuple-element.169) | copy-start | bytes 12292
  334.7 18.8 %copy-start.45 = (f32[2,512]{1,0:T(2,128)}, f32[2,512]{1,0:T(2,128)S(1)}, u32[]{:S(2)}) copy-start(f32[2,512]{1,0:T(2,128)S(1)} %get-tuple-element.168) | copy-start | bytes 12292
  337.1 16.4 %copy-start.52 = (f32[2,512]{1,0:T(2,128)}, f32[2,512]{1,0:T(2,128)S(1)}, u32[]{:S(2)}) copy-start(f32[2,512]{1,0:T(2,128)S(1)} %negate_multiply_fusion.2) | copy-start | bytes 12292
  353.5 11.2 %copy-start.3 = (f32[2,512,768]{2,1,0:T(8,128)S(1)}, f32[2,512,768]{2,1,0:T(8,128)}, u32[]{:S(2)}) copy-start(f32[2,512,768]{2,1,0:T(8,128)} %copy-done.2) | copy-start | bytes 9437188
  365.9 2.8 copy-start.11
  366.0 2.8 copy-start.55
  368.7 231.6 %reduce-scatter.6.cloned.1.call-start = ((), (), s32[]{:S(2)}) async-start(), calls=%async_computation.10 | async-start | bytes 1327104 | tf_op jit(solution)/shard_map/reduce_scatter | solution.py:305
  372.6 77.6 %copy-start.56 = (f32[2,512]{1,0:T(2,128)S(1)}, f32[2,512]{1,0:T(2,128)}, u32[]{:S(2)}) copy-start(f32[2,512]{1,0:T(2,128)} %copy-done.55) | copy-start | bytes 12292
  375.1 6.4 copy-start.10
  383.9 11.6 %slice-start = ((s8[12582912]{0:T(1024)(128)(4,1)}), s8[4194304]{0:T(1024)(128)(4,1)S(1)}, s32[]{:S(2)}) async-start(s8[12582912]{0:T(1024)(128)(4,1)} %bitcast.161), calls=%async_computation.16 | async-start | bytes 8388608 | tf_op jit(solution)/shard_map/while
  383.9 11.5 %slice-start.1 = ((s8[12582912]{0:T(1024)(128)(4,1)}), s8[4194304]{0:T(1024)(128)(4,1)S(1)}, s32[]{:S(2)}) async-start(s8[12582912]{0:T(1024)(128)(4,1)} %bitcast.161), calls=%async_computation.17 | async-start | bytes 8388608 | tf_op jit(solution)/shard_map/while
  383.9 12.8 %slice-start.2 = ((s8[12582912]{0:T(1024)(128)(4,1)}), s8[4194304]{0:T(1024)(128)(4,1)S(1)}, s32[]{:S(2)}) async-start(s8[12582912]{0:T(1024)(128)(4,1)} %bitcast.161), calls=%async_computation.18 | async-start | bytes 8388608 | tf_op jit(solution)/shard_map/while
  413.6 6.4 copy-start.10
  422.4 11.5 %slice-start = ((s8[12582912]{0:T(1024)(128)(4,1)}), s8[4194304]{0:T(1024)(128)(4,1)S(1)}, s32[]{:S(2)}) async-start(s8[12582912]{0:T(1024)(128)(4,1)} %bitcast.161), calls=%async_computation.16 | async-start | bytes 8388608 | tf_op jit(solution)/shard_map/while
  422.4 11.5 %slice-start.1 = ((s8[12582912]{0:T(1024)(128)(4,1)}), s8[4194304]{0:T(1024)(128)(4,1)S(1)}, s32[]{:S(2)}) async-start(s8[12582912]{0:T(1024)(128)(4,1)} %bitcast.161), calls=%async_computation.17 | async-start | bytes 8388608 | tf_op jit(solution)/shard_map/while
  422.4 12.7 %slice-start.2 = ((s8[12582912]{0:T(1024)(128)(4,1)}), s8[4194304]{0:T(1024)(128)(4,1)S(1)}, s32[]{:S(2)}) async-start(s8[12582912]{0:T(1024)(128)(4,1)} %bitcast.161), calls=%async_computation.18 | async-start | bytes 8388608 | tf_op jit(solution)/shard_map/while
  450.2 10.2 %copy-start.5 = (f32[2,128,768]{2,1,0:T(8,128)S(1)}, f32[2,128,768]{2,1,0:T(8,128)}, u32[]{:S(2)}) copy-start(f32[2,128,768]{2,1,0:T(8,128)} %copy-done.4) | copy-start | bytes 2359300
  450.2 10.2 %copy-start.25 = (f32[768]{0:T(1024)S(1)}, f32[768]{0:T(1024)}, u32[]{:S(2)}) copy-start(f32[768]{0:T(1024)} %copy-done.24) | copy-start | bytes 9220
  450.2 10.2 %copy-start.31 = (s32[2,512]{1,0:T(2,128)S(1)}, s32[2,512]{1,0:T(2,128)}, u32[]{:S(2)}) copy-start(s32[2,512]{1,0:T(2,128)} %param.33) | copy-start | bytes 12292
  450.2 10.1 %copy-start.33 = (f32[768]{0:T(1024)S(1)}, f32[768]{0:T(1024)}, u32[]{:S(2)}) copy-start(f32[768]{0:T(1024)} %copy-done.32) | copy-start | bytes 9220
  460.4 40.6 %copy-start.35 = (f32[768]{0:T(1024)S(1)}, f32[768]{0:T(1024)}, u32[]{:S(2)}) copy-start(f32[768]{0:T(1024)} %copy-done.34) | copy-start | bytes 9220
  460.4 40.6 %copy-start.48 = (f32[2,128]{1,0:T(2,128)S(1)}, f32[2,128]{1,0:T(2,128)}, u32[]{:S(2)}) copy-start(f32[2,128]{1,0:T(2,128)} %copy-done.47) | copy-start | bytes 3076
  460.4 42.3 %copy-start.17 = (bf16[2,128,768]{2,1,0:T(8,128)(2,1)S(1)}, bf16[2,128,768]{2,1,0:T(8,128)(2,1)}, u32[]{:S(2)}) copy-start(bf16[2,128,768]{2,1,0:T(8,128)(2,1)} %copy-done.16) | copy-start | bytes 1179652
  502.7 2.3 copy-start.7
  504.3 146.8 %reduce-scatter.8.cloned.1.call-start = ((), (), s32[]{:S(2)}) async-start(), calls=%async_computation.11 | async-start | bytes 3981312 | tf_op jit(solution)/shard_map/reduce_scatter | solution.py:308
  513.5 1.9 copy-start.1
  513.5 1.9 copy-start.27
  513.5 1.9 copy-start.29
  513.5 1.9 copy-start.39
  513.5 1.9 copy-start.46
  513.6 236.1 %reduce-scatter.14.cloned.1.call-start = ((), (), s32[]{:S(2)}) async-start(), calls=%async_computation.14 | async-start | bytes 5308416 | tf_op jit(solution)/shard_map/reduce_scatter | solution.py:323
  526.6 321.6 %reduce-scatter.12.cloned.1.call-start = ((), (), s32[]{:S(2)}) async-start(), calls=%async_computation.13 | async-start | bytes 5308416 | tf_op jit(solution)/shard_map/reduce_scatter | solution.py:320
  537.8 310.5 %copy-start.19 = (bf16[2,128,768]{2,1,0:T(8,128)(2,1)S(1)}, bf16[2,128,768]{2,1,0:T(8,128)(2,1)}, u32[]{:S(2)}) copy-start(bf16[2,128,768]{2,1,0:T(8,128)(2,1)} %copy-done.18) | copy-start | bytes 1179652
  537.8 362.3 %all-reduce.18.cloned.1.call-start = ((), (), s32[]{:S(2)}) async-start(), calls=%async_computation.15 | async-start | bytes 3833856 | tf_op jit(solution)/shard_map/psum | solution.py:334
  850.1 2.9 copy-start.9
  900.2 4.4 copy-start.20
  900.2 5.4 copy-start.22
  900.2 6.1 copy-start.21
  (12 other events, 12.7 us)
Sparse Core Ops, SparseCore 0:
  10.2 44.0 all-gather.5
  56.5 64.8 all-gather.7
  123.5 39.6 all-gather.9
  165.3 78.6 all-gather.11
  246.0 78.0 all-gather.13
  368.8 62.2 reduce-scatter.9
  504.4 64.7 reduce-scatter.5
  572.9 78.1 reduce-scatter.7
  654.7 94.9 reduce-scatter.13
  753.2 95.0 reduce-scatter.11
  851.0 49.1 all-reduce.17
where the time goes:
time: 922 us; the launch traced here: 914 us
  waiting for transfers between devices  378 us (41%)
  blocking collectives  202 us (22%)
  matrix products  186 us (20%)
  other arithmetic  84 us (9%)
  local copies, waits for them, and re-layouts  44.5 us (5%)
  between operations  16.8 us (2%)
    reduce_scatter x1, waiting for transfers between devices, shards(): lax.psum_scatter(down_local.astype(jnp.bfloat16), 'fsdp', scatter_dimensi...  98.7 us
    reduce_scatter x1, waiting for transfers between devices, shards(): lax.psum_scatter(up_local.astype(jnp.bfloat16), 'fsdp', scatter_dimension...  98.5 us
    unnamed x2, blocking collectives  76.1 us
    reduce_scatter x1, waiting for transfers between devices, shards(): lax.psum_scatter(attend_local.astype(jnp.bfloat16), 'fsdp', scatter_dimen...  50.8 us
    all_gather x1, waiting for transfers between devices, shards(): lax.all_gather(up_matrix, 'fsdp', axis=0, tiled=True)  48.8 us
    psum x1, waiting for transfers between devices, shards(): lax.psum(visual_shard.astype(jnp.bfloat16), 'dp').astype(jnp.float32)  44 us
    psum x1, blocking collectives, shards(): lax.psum(jnp.sum(valid_slot * center * center, axis=(0, 1)), ('dp', 'fsdp'))  42.7 us
    psum x1, blocking collectives, shards(): lax.psum((jnp.sum(delta_embedded, axis=(0, 1)), jnp.sum(delta_embedded *...  38.4 us
  transfers between devices with their start and end apart: 11, of which 6 were waited for; matrix products, arithmetic and copies ran while one was open for 28% of the time, Pallas kernels for 0%

commit v1 on v0

--- a/solution.py
+++ b/solution.py
@@ -331,7 +331,9 @@
         ).astype(jnp.float32),
     )
     summed = (
-        lax.psum(visual_shard.astype(jnp.bfloat16), "dp").astype(jnp.float32),
+        jnp.sum(lax.all_gather(visual_shard.astype(jnp.bfloat16), "dp"), axis=0).astype(
+            jnp.float32
+        ),
         lax.psum(attend_shard.astype(jnp.bfloat16), "dp").astype(jnp.float32),
         lax.psum(merge_shard.astype(jnp.bfloat16), "dp").astype(jnp.float32),
         lax.psum(first_gain_shard.astype(jnp.bfloat16), "dp").astype(jnp.float32),

time: 922 us -> 872 us (0.946)
  waiting for transfers between devices: 378 us -> 326 us
  blocking collectives: 202 us -> 212 us
    reduce_scatter x1, waiting for transfers between devices: 0.01 us -> 62.7 us  [shards(): lax.psum_scatter(visual_local.astype(jnp.bfloat16), 'fsdp', scatter_dimen...]
    reduce_scatter x1, waiting for transfers between devices: 98.7 us -> 39 us  [shards(): lax.psum_scatter(down_local.astype(jnp.bfloat16), 'fsdp', scatter_dimensi...]
    reduce_scatter x1, waiting for transfers between devices: 50.8 us -> 0.01 us  [shards(): lax.psum_scatter(attend_local.astype(jnp.bfloat16), 'fsdp', scatter_dimen...]
    unnamed x131 -> x119, local copies, waits for them, and re-layouts: 19.9 us -> 11.9 us
  transfers between devices with their start and end apart: 11 -> 11, of which waited for: 6 -> 6; matrix products, arithmetic and copies ran while one was open for 28% -> 29% of each run, Pallas kernels for 0% -> 0%
where the time goes in v1:
time: 872 us; the launch traced here: 864 us
  waiting for transfers between devices  326 us (37%)
  blocking collectives  212 us (24%)
  matrix products  189 us (22%)
  other arithmetic  81.6 us (9%)
  local copies, waits for them, and re-layouts  36.6 us (4%)
  between operations  16.8 us (2%)
    reduce_scatter x1, waiting for transfers between devices, shards(): lax.psum_scatter(up_local.astype(jnp.bfloat16), 'fsdp', scatter_dimension...  98.8 us
    unnamed x2, blocking collectives  78.2 us
    reduce_scatter x1, waiting for transfers between devices, shards(): lax.psum_scatter(visual_local.astype(jnp.bfloat16), 'fsdp', scatter_dimen...  62.7 us
    all_gather x1, waiting for transfers between devices, shards(): lax.all_gather(up_matrix, 'fsdp', axis=0, tiled=True)  48.8 us
    psum x1, blocking collectives, shards(): lax.psum(jnp.sum(valid_slot * center * center, axis=(0, 1)), ('dp', 'fsdp'))  42.7 us
    psum x1, waiting for transfers between devices, shards(): lax.psum(attend_shard.astype(jnp.bfloat16), 'dp').astype(jnp.float32)  39.7 us
    psum x1, blocking collectives, shards(): lax.psum((jnp.sum(delta_embedded, axis=(0, 1)), jnp.sum(delta_embedded *...  39.3 us
    reduce_scatter x1, waiting for transfers between devices, shards(): lax.psum_scatter(down_local.astype(jnp.bfloat16), 'fsdp', scatter_dimensi...  39 us
  transfers between devices with their start and end apart: 11, of which 6 were waited for; matrix products, arithmetic and copies ran while one was open for 29% of the time, Pallas kernels for 0%

profile of v1, /device:TPU:0, one launch (start us, length us, event | category | flops | bytes accessed | tf_op | source)
XLA Modules:
  0.0 864.1 jit_solution(16278802420608402457)
XLA Ops:
  20.4 39.1 %all-reduce.13 = (bf16[768]{0:T(1024)(128)(2,1)S(1)}, bf16[768]{0:T(1024)(128)(2,1)S(1)}, bf16[768]{0:T(1024)(128)(2,1)S(1)}, bf16[768]{0:T(1024)(128)(2,1)S(1)}, bf16[768]{0:T(1024)(128)(2,1)S(1)}) all-reduce(bf16[768]{0:T(1024)(128)(2,1)S(1)} %dynamic-update-slice.1, ...), channel_id=1, replica_groups=mesh['dp'=4,'fsdp'=8] {'fsdp'}, use_global_device_ids=true, to_apply=%add.1 | all-reduce | flops 3840 | bytes 15360
  61.3 2.1 fusion.47
  63.5 2.0 multiply_reduce_fusion.6
  65.6 38.1 %all-reduce.11 = (f32[768]{0:T(1024)S(1)}, f32[]{:T(128)}) all-reduce(f32[768]{0:T(1024)S(1)} %get-tuple-element.171, f32[]{:T(128)S(6)} %convert_element_type.183), channel_id=1, replica_groups=mesh['dp'=4,'fsdp'=8] {'dp','fsdp'}, use_global_device_ids=true, to_apply=%region_2.0 | all-reduce | flops 769 | bytes 6152 | tf_op jit(solution)/shard_map/psum | solution.py:157
  104.5 42.7 %psum.93 = f32[768]{0:T(1024)S(1)} all-reduce(f32[768]{0:T(1024)S(1)} %fusion.53), channel_id=1, replica_groups=mesh['dp'=4,'fsdp'=8] {'dp','fsdp'}, use_global_device_ids=true, to_apply=%region_6.0 | all-reduce | flops 768 | bytes 6144 | tf_op jit(solution)/shard_map/psum | solution.py:163
  147.8 2.3 fusion.55
  150.1 8.9 %convolution_convert_fusion = bf16[2,512,2304]{2,1,0:T(8,128)(2,1)} fusion(bf16[768,2304]{1,0:T(8,128)(2,1)} %all-gather.9.cloned.1.call-done, f32[2,512,768]{2,1,0:T(8,128)} %fusion.55, bf16[2,512,768]{2,1,0:T(8,128)(2,1)S(1)} %copy-done.11), kind=kOutput, calls=%fused_computation.53 | convolution fusion | flops 3628597248 | bytes 12976128 | tf_op jit(solution)/shard_map/drc,ce->dre/dot_general | solution.py:174
  159.1 6.8 copy.50
  165.9 22.8 %while.22 = (s32[]{:T(128)}, bf16[2,512,768]{1,2,0:T(8,128)(2,1)S(1)}, f32[2,12,512]{2,1,0:T(8,128)S(1)}, bf16[2,512,2304]{1,2,0:T(8,128)(2,1)}, s32[2,512]{1,0:T(2,128)S(1)}, /*index=5*/s32[]{:T(128)}) while((s32[]{:T(128)}, bf16[2,512,768]{1,2,0:T(8,128)(2,1)S(1)}, f32[2,12,512]{2,1,0:T(8,128)S(1)}, bf16[2,512,2304]{1,2,0:T(8,128)(2,1)}, ...), condition=%wide.region_10.11_spmd, body=%wide.region_7.10_spmd.sunk | while | flops 843442688 | bytes 52129876 | solution.py:177
  166.4 1.8 dynamic-slice_bitcast_fusion.6
  168.4 3.1 fusion.131
  171.5 2.6 fusion.132
  174.1 3.3 fusion.133
  177.5 1.8 dynamic-slice_bitcast_fusion.6
  179.5 3.1 fusion.131
  182.6 2.6 fusion.132
  185.2 3.3 fusion.133
  189.9 4.8 fusion.77
  195.2 48.8 %all-gather.13.cloned.1.call-done = bf16[768,3072]{1,0:T(8,128)(2,1)} async-done(((bf16[96,3072]{1,0:T(8,128)(2,1)}), bf16[768,3072]{1,0:T(8,128)(2,1)}) %all-gather.13.cloned.1.call-update) | async-done | bytes 4718608 | tf_op jit(solution)/shard_map/all_gather | solution.py:124
  244.0 14.9 %fusion.36 = (u8[512,3072]{1,0:T(8,128)(4,1)S(1)}, u8[512,3072]{1,0:T(8,128)(4,1)S(1)}, f32[2,512,3072]{2,1,0:T(8,128)}) fusion(bf16[768,3072]{1,0:T(8,128)(2,1)} %all-gather.13.cloned.1.call-done, f32[2,512,768]{2,1,0:T(8,128)S(1)} %get-tuple-element.174, f32[768]{0:T(1024)S(1)} %copy-done.45, f32[768]{0:T(1024)S(1)} %copy-done.38, ...), kind=kOutput, calls=%fused_computation.80 | convolution fusion | flops 4873519104 | bytes 23607296 | tf_op jit(solution)/shard_map/sjq,qy->sjy/dot_general | solution.py:184
  258.9 31.0 %multiply_convert_fusion.3 = (bf16[2,512,3072]{2,1,0:T(8,128)(2,1)}, f32[2,512,3072]{2,1,0:T(8,128)}) fusion(f32[2,512,3072]{2,1,0:T(8,128)} %get-tuple-element.175, u8[512,3072]{1,0:T(8,128)(4,1)S(1)} %get-tuple-element.99, u8[512,3072]{1,0:T(8,128)(4,1)S(1)} %get-tuple-element.98), kind=kLoop, calls=%fused_computation.37 | loop fusion | flops 220200960 | bytes 34603008 | tf_op jit(solution)/shard_map/convert_element_type | solution.py:190
  289.9 34.1 %all-gather.15.cloned.1.call-done = bf16[3072,768]{1,0:T(8,128)(2,1)} async-done(((bf16[384,768]{1,0:T(8,128)(2,1)}), bf16[3072,768]{1,0:T(8,128)(2,1)}) %all-gather.15.cloned.1.call-update) | async-done | bytes 4718608 | tf_op jit(solution)/shard_map/all_gather | solution.py:125
  324.1 9.5 %fusion.78 = (f32[2,512]{1,0:T(2,128)S(1)}, f32[2,512,768]{2,1,0:T(8,128)S(1)}) fusion(bf16[2,512,3072]{2,1,0:T(8,128)(2,1)} %get-tuple-element.155, bf16[3072,768]{1,0:T(8,128)(2,1)} %all-gather.15.cloned.1.call-done, f32[768]{0:T(1024)S(1)} %copy-done.45, f32[768]{0:T(1024)S(1)} %copy-done.38, f32[2,512]{1,0:T(2,128)S(1)} %fusion.66, ...), kind=kOutput, calls=%fused_computation.142 | convolution fusion | flops 4836555776 | bytes 17319936 | tf_op jit(solution)/shard_map/zya,av->zyv/dot_general | solution.py:191
  334.7 2.4 fusion.34
  337.1 16.4 %add_convert_fusion = bf16[2,512,3072]{2,1,0:T(8,128)(2,1)} fusion(f32[2,512,3072]{2,1,0:T(8,128)} %get-tuple-element.156, f32[2,512,3072]{2,1,0:T(8,128)} %get-tuple-element.175, bf16[3072,768]{1,0:T(8,128)(2,1)} %all-gather.15.cloned.1.call-done, f32[2,512]{1,0:T(2,128)S(1)} %negate_multiply_fusion.2, bf16[2,512,768]{2,1,0:T(8,128)(2,1)} %param.35, ...), kind=kOutput, calls=%fused_computation.36 | convolution fusion | flops 4882956288 | bytes 40913920 | tf_op jit(solution)/shard_map/ivj,hj->ivh/dot_general | solution.py:229
  353.5 11.2 %multiply_reduce_fusion.1 = (bf16[768]{0:T(1024)(128)(2,1)}, f32[2,512]{1,0:T(2,128)S(1)}, bf16[768]{0:T(1024)(128)(2,1)}, f32[2,512,768]{2,1,0:T(8,128)S(1)}) fusion(f32[2,512,768]{2,1,0:T(8,128)} %copy-done.2, f32[2,512]{1,0:T(2,128)S(1)} %fusion.66, f32[2,512]{1,0:T(2,128)S(1)} %broadcast_multiply_fusion.1, f32[768]{0:T(1024)S(1)} %copy-done.38, ...), kind=kOutput, calls=%fused_computation.72 | convolution fusion | flops 4845204480 | bytes 22057984 | tf_op jit(solution)/shard_map/wmx,ix->wmi/dot_general | solution.py:237
  366.2 2.5 bitcast_convert_fusion.3
  368.8 3.9 convolution_convert_fusion.1
  372.7 77.6 %while.23 = (s32[]{:T(128)}, bf16[2,512,2304]{1,2,0:T(8,128)(2,1)}, bf16[2,512,2304]{1,2,0:T(8,128)(2,1)}, s32[2,512]{1,0:T(2,128)S(1)}, f32[2,12,512]{2,1,0:T(8...) while((s32[]{:T(128)}, bf16[2,512,2304]{1,2,0:T(8,128)(2,1)}, bf16[2,512,2304]{1,2,0:T(8,128)(2,1)}, ...), condition=%wide.region_21.22_spmd, body=%wide.region_19.21_spmd.sunk | while | flops 2069490176 | bytes 163754704 | solution.py:254
  373.1 1.9 dynamic-slice_bitcast_fusion.7
  375.2 6.4 fusion.145
  384.0 11.5 %multiply_reduce_fusion.8 = (f32[12,512]{1,0:T(8,128)S(1)}, f32[12,512,512]{1,2,0:T(8,128)}) fusion(f32[12,512,512]{1,2,0:T(8,128)} %fusion.145, f32[12,512]{1,0:T(8,128)S(1)} %dynamic-slice_bitcast_fusion.8, pred[512]{0:T(512)(128)(4,1)S(1)} %compare_reduce_fusion.5, bf16[512,12,64]{0,2,1:T(8,128)(2,1)S(1)} %bitcast.170, ...), kind=kOutput, calls=%fused_computation.14.clone.1 | convolution fusion | flops 418375680 | bytes 26788352 | tf_op jit(solution)/shard_map/while/body/eval_jaxpr/qhe,khe->hqk/dot_general | solution.py:67
  396.8 7.1 multiply_convert_fusion.8
  405.1 2.0 multiply_convert_fusion.9
  407.1 3.1 fusion.146
  410.2 1.6 maximum_dynamic-update-slice_fusion.2
  411.8 1.8 dynamic-slice_bitcast_fusion.7
  413.8 6.4 fusion.145
  422.6 11.5 %multiply_reduce_fusion.8 = (f32[12,512]{1,0:T(8,128)S(1)}, f32[12,512,512]{1,2,0:T(8,128)}) fusion(f32[12,512,512]{1,2,0:T(8,128)} %fusion.145, f32[12,512]{1,0:T(8,128)S(1)} %dynamic-slice_bitcast_fusion.8, pred[512]{0:T(512)(128)(4,1)S(1)} %compare_reduce_fusion.5, bf16[512,12,64]{0,2,1:T(8,128)(2,1)S(1)} %bitcast.170, ...), kind=kOutput, calls=%fused_computation.14.clone.1 | convolution fusion | flops 418375680 | bytes 26788352 | tf_op jit(solution)/shard_map/while/body/eval_jaxpr/qhe,khe->hqk/dot_general | solution.py:67
  435.3 7.1 multiply_convert_fusion.8
  443.5 2.0 multiply_convert_fusion.9
  445.5 3.1 fusion.146
  448.6 1.6 maximum_dynamic-update-slice_fusion.2
  450.4 9.4 %bitcast_convert_fusion.2 = bf16[768,2304]{1,0:T(8,128)(2,1)} fusion(bf16[2,512,2304]{1,2,0:T(8,128)(2,1)} %get-tuple-element.75, f32[2,512,768]{2,1,0:T(8,128)} %fusion.55, bf16[2,512,768]{2,1,0:T(8,128)(2,1)} %param.20), kind=kOutput, calls=%fused_computation.52 | convolution fusion | flops 3628007424 | bytes 12976128 | tf_op jit(solution)/shard_map/drc,dre->ce/dot_general | solution.py:255
  459.9 1.8 copy-done.1
  461.7 11.2 %bitcast_convert_fusion = bf16[3072,768]{1,0:T(8,128)(2,1)} fusion(bf16[2,512,3072]{2,1,0:T(8,128)(2,1)} %get-tuple-element.155, f32[2,512]{1,0:T(2,128)S(1)} %copy-done.50, bf16[2,512,768]{2,1,0:T(8,128)(2,1)} %param.35, f32[2,512,768]{2,1,0:T(8,128)S(1)} %copy-done.1, f32[2,512]{1,0:T(2,128)S(1)} %copy-done.43, f32[768]{0:T(1024)S(1)} %copy-done.25, ...), kind=kOutput, calls=%fused_computation.50 | convolution fusion | flops 4841275392 | bytes 15748096 | tf_op jit(solution)/shard_map/omt,oms->ts/dot_general | solution.py:226
  473.6 10.7 %bitcast_convert_fusion.1 = bf16[768,3072]{1,0:T(8,128)(2,1)} fusion(bf16[2,512,3072]{2,1,0:T(8,128)(2,1)} %add_convert_fusion, f32[2,512,768]{2,1,0:T(8,128)} %copy-done.2, f32[768]{0:T(1024)S(1)} %copy-done.46, f32[768]{0:T(1024)S(1)} %copy-done.39, f32[2,512]{1,0:T(2,128)S(1)} %copy-done.41, f32[2,512]{1,0:T(2,128)S(1)} %copy-done.34), kind=kOutput, calls=%fused_computation.51 | convolution fusion | flops 4838129664 | bytes 14170112 | tf_op jit(solution)/shard_map/oih,oiu->hu/dot_general | solution.py:234
  484.9 8.6 add_add_fusion.2
  493.6 3.0 fusion.71
  496.6 39.3 %all-reduce.10 = (f32[768]{0:T(1024)}, f32[768]{0:T(1024)}) all-reduce(f32[768]{0:T(1024)} %get-tuple-element.108, f32[768]{0:T(1024)} %get-tuple-element.107), channel_id=1, replica_groups=mesh['dp'=4,'fsdp'=8] {'dp','fsdp'}, use_global_device_ids=true, to_apply=%region_25.26 | all-reduce | flops 1536 | bytes 12288 | tf_op jit(solution)/shard_map/psum | solution.py:268
  537.2 2.3 multiply_convert_fusion.4
  541.8 1.7 reduce_sum.227
  547.6 39.1 %all-reduce.12 = (bf16[768]{0:T(1024)(128)(2,1)S(1)}, bf16[768]{0:T(1024)(128)(2,1)S(1)}, bf16[768]{0:T(1024)(128)(2,1)S(1)}, bf16[768]{0:T(1024)(128)(2,1)S(1)}, bf16[768]{0:T(1024)(128)(2,1)S(1)}) all-reduce(bf16[768]{0:T(1024)(128)(2,1)S(1)} %dynamic-update-slice.5, ...), channel_id=1, replica_groups=mesh['dp'=4,'fsdp'=8] {'fsdp'}, use_global_device_ids=true, to_apply=%add.5 | all-reduce | flops 3840 | bytes 15360
  587.0 6.3 all-reduce.14
  595.4 2.2 multiply_add_fusion
  597.6 39.0 %reduce-scatter.14.cloned.1.call-done = bf16[384,768]{1,0:T(8,128)(2,1)} async-done(((bf16[3072,768]{1,0:T(8,128)(2,1)}), bf16[384,768]{1,0:T(8,128)(2,1)}) %reduce-scatter.14.cloned.1.call-update) | async-done | bytes 589840 | tf_op jit(solution)/shard_map/reduce_scatter | solution.py:323
  636.5 98.8 %reduce-scatter.12.cloned.1.call-done = bf16[96,3072]{1,0:T(8,128)(2,1)} async-done(((bf16[768,3072]{1,0:T(8,128)(2,1)}), bf16[96,3072]{1,0:T(8,128)(2,1)}) %reduce-scatter.12.cloned.1.call-update) | async-done | bytes 589840 | tf_op jit(solution)/shard_map/reduce_scatter | solution.py:320
  735.4 1.8 convolution_divide_fusion
  737.2 3.1 convolution_add_fusion
  740.3 62.7 %reduce-scatter.6.cloned.1.call-done = bf16[96,768]{1,0:T(8,128)(2,1)} async-done(((bf16[768,768]{1,0:T(8,128)(2,1)}), bf16[96,768]{1,0:T(8,128)(2,1)}) %reduce-scatter.6.cloned.1.call-update) | async-done | bytes 147472 | tf_op jit(solution)/shard_map/reduce_scatter | solution.py:305
  803.0 7.7 all-gather
  811.5 39.7 %all-reduce.18.cloned.1.call-done = (bf16[96,2304]{1,0:T(8,128)(2,1)}, bf16[96,768]{1,0:T(8,128)(2,1)}, bf16[96,3072]{1,0:T(8,128)(2,1)}, bf16[384,768]{1,0:T(8,128)(2,1)}) async-done(((bf16[96,2304]{1,0:T(8,128)(2,1)}, bf16[96,768]{1,0:T(8,128)(2,1)}, bf16[96,3072]{1,0:T(8,128)(2,1)}, bf16[384,768]{1,0:T(8,128)(2,1)}), (bf16[96,2304]{1,0:T(8,128)(2,1)}, bf16[96,768]{1,0:T(8,128)(2,1)}, ...) | async-done | bytes 1769488 | tf_op jit(solution)/shard_map/psum | solution.py:337
  851.2 2.2 convert_element_type.212
  853.5 2.2 convert_element_type.214
  (221 shorter events, 43.1 us)
Async XLA Ops:
  7.2 56.3 %all-gather.7.cloned.1.call-start = ((), (), s32[]{:S(2)}) async-start(), calls=%async_computation.5 | async-start | bytes 1327104 | tf_op jit(solution)/shard_map/all_gather | solution.py:117
  7.9 142.2 %all-gather.9.cloned.1.call-start = ((), (), s32[]{:S(2)}) async-start(), calls=%async_computation.6 | async-start | bytes 3981312 | tf_op jit(solution)/shard_map/all_gather | solution.py:120
  8.7 180.1 %all-gather.11.cloned.1.call-start = ((), (), s32[]{:S(2)}) async-start(), calls=%async_computation.7 | async-start | bytes 1327104 | tf_op jit(solution)/shard_map/all_gather | solution.py:121
  9.4 234.6 %all-gather.13.cloned.1.call-start = ((), (), s32[]{:S(2)}) async-start(), calls=%async_computation.8 | async-start | bytes 5308416 | tf_op jit(solution)/shard_map/all_gather | solution.py:124
  10.0 314.1 %all-gather.15.cloned.1.call-start = ((), (), s32[]{:S(2)}) async-start(), calls=%async_computation.9 | async-start | bytes 5308416 | tf_op jit(solution)/shard_map/all_gather | solution.py:125
  10.6 587.0 %reduce-scatter.10.cloned.1.call-start = ((), (), s32[]{:S(2)}) async-start(), calls=%async_computation.12 | async-start | bytes 1327104 | tf_op jit(solution)/shard_map/reduce_scatter | solution.py:311
  11.4 92.9 %copy-start.44 = (f32[2,128]{1,0:T(2,128)}, f32[2,128]{1,0:T(2,128)S(1)}, u32[]{:S(2)}) copy-start(f32[2,128]{1,0:T(2,128)S(1)} %compare_convert_fusion) | copy-start | bytes 3076
  13.6 49.9 %copy-start.51 = (f32[2,128]{1,0:T(2,128)}, f32[2,128]{1,0:T(2,128)S(1)}, u32[]{:S(2)}) copy-start(f32[2,128]{1,0:T(2,128)S(1)} %broadcast_maximum_fusion) | copy-start | bytes 3076
  59.5 88.3 %copy-start.32 = (f32[768]{0:T(1024)}, f32[768]{0:T(1024)S(1)}, u32[]{:S(2)}) copy-start(f32[768]{0:T(1024)S(1)} %convert_element_type.184) | copy-start | bytes 9220
  61.3 86.5 %copy-start.28 = (s32[2,512]{1,0:T(2,128)S(1)}, s32[2,512]{1,0:T(2,128)}, u32[]{:S(2)}) copy-start(s32[2,512]{1,0:T(2,128)} %param.33) | copy-start | bytes 12292
  63.4 86.7 %copy-start.15 = (bf16[2,128,768]{2,1,0:T(8,128)(2,1)}, bf16[2,128,768]{2,1,0:T(8,128)(2,1)S(1)}, u32[]{:S(2)}) copy-start(bf16[2,128,768]{2,1,0:T(8,128)(2,1)S(1)} %fusion.47) | copy-start | bytes 1179652
  63.5 86.7 %copy-start.11 = (bf16[2,512,768]{2,1,0:T(8,128)(2,1)S(1)}, bf16[2,512,768]{2,1,0:T(8,128)(2,1)}, u32[]{:S(2)}) copy-start(bf16[2,512,768]{2,1,0:T(8,128)(2,1)} %param.20) | copy-start | bytes 4718596
  65.5 93.5 %copy-start.4 = (f32[2,128,768]{2,1,0:T(8,128)}, f32[2,128,768]{2,1,0:T(8,128)S(1)}, u32[]{:S(2)}) copy-start(f32[2,128,768]{2,1,0:T(8,128)S(1)} %get-tuple-element.172) | copy-start | bytes 2359300
  104.3 54.8 %copy-start.22 = (f32[768]{0:T(1024)}, f32[768]{0:T(1024)S(1)}, u32[]{:S(2)}) copy-start(f32[768]{0:T(1024)S(1)} %broadcast_divide_fusion.1) | copy-start | bytes 9220
  147.8 11.2 %copy-start.30 = (f32[768]{0:T(1024)}, f32[768]{0:T(1024)S(1)}, u32[]{:S(2)}) copy-start(f32[768]{0:T(1024)S(1)} %add_rsqrt_fusion) | copy-start | bytes 9220
  159.1 6.8 copy-start.12
  159.1 6.8 copy-start.21
  188.7 1.2 copy-start.13
  194.6 64.2 %copy-start.2 = (f32[2,512,768]{2,1,0:T(8,128)}, f32[2,512,768]{2,1,0:T(8,128)S(1)}, u32[]{:S(2)}) copy-start(f32[2,512,768]{2,1,0:T(8,128)S(1)} %get-tuple-element.174) | copy-start | bytes 9437188
  194.6 49.3 %copy-start.38 = (f32[768]{0:T(1024)S(1)}, f32[768]{0:T(1024)}, u32[]{:S(2)}) copy-start(f32[768]{0:T(1024)} %convert_element_type.189) | copy-start | bytes 9220
  194.6 49.3 %copy-start.45 = (f32[768]{0:T(1024)S(1)}, f32[768]{0:T(1024)}, u32[]{:S(2)}) copy-start(f32[768]{0:T(1024)} %convert_element_type.190) | copy-start | bytes 9220
  194.7 170.1 %copy-start.33 = (f32[2,512]{1,0:T(2,128)}, f32[2,512]{1,0:T(2,128)S(1)}, u32[]{:S(2)}) copy-start(f32[2,512]{1,0:T(2,128)S(1)} %broadcast_multiply_fusion.1) | copy-start | bytes 12292
  195.2 169.6 %copy-start.40 = (f32[2,512]{1,0:T(2,128)}, f32[2,512]{1,0:T(2,128)S(1)}, u32[]{:S(2)}) copy-start(f32[2,512]{1,0:T(2,128)S(1)} %fusion.66) | copy-start | bytes 12292
  324.1 9.6 %copy-start.6 = (bf16[2,512,768]{2,1,0:T(8,128)(2,1)S(1)}, bf16[2,512,768]{2,1,0:T(8,128)(2,1)}, u32[]{:S(2)}) copy-start(bf16[2,512,768]{2,1,0:T(8,128)(2,1)} %param.35) | copy-start | bytes 4718596
  324.1 9.6 %copy-start.24 = (f32[768]{0:T(1024)S(1)}, f32[768]{0:T(1024)}, u32[]{:S(2)}) copy-start(f32[768]{0:T(1024)} %convert_element_type.193) | copy-start | bytes 9220
  333.6 19.9 %copy-start = (f32[2,512,768]{2,1,0:T(8,128)}, f32[2,512,768]{2,1,0:T(8,128)S(1)}, u32[]{:S(2)}) copy-start(f32[2,512,768]{2,1,0:T(8,128)S(1)} %get-tuple-element.177) | copy-start | bytes 9437188
  333.6 19.8 %copy-start.26 = (f32[2,512]{1,0:T(2,128)}, f32[2,512]{1,0:T(2,128)S(1)}, u32[]{:S(2)}) copy-start(f32[2,512]{1,0:T(2,128)S(1)} %broadcast_multiply_fusion) | copy-start | bytes 12292
  334.7 18.8 %copy-start.35 = (f32[2,512]{1,0:T(2,128)}, f32[2,512]{1,0:T(2,128)S(1)}, u32[]{:S(2)}) copy-start(f32[2,512]{1,0:T(2,128)S(1)} %get-tuple-element.168) | copy-start | bytes 12292
  334.7 18.8 %copy-start.42 = (f32[2,512]{1,0:T(2,128)}, f32[2,512]{1,0:T(2,128)S(1)}, u32[]{:S(2)}) copy-start(f32[2,512]{1,0:T(2,128)S(1)} %get-tuple-element.167) | copy-start | bytes 12292
  337.1 16.4 %copy-start.49 = (f32[2,512]{1,0:T(2,128)}, f32[2,512]{1,0:T(2,128)S(1)}, u32[]{:S(2)}) copy-start(f32[2,512]{1,0:T(2,128)S(1)} %negate_multiply_fusion.2) | copy-start | bytes 12292
  353.5 11.3 %copy-start.3 = (f32[2,512,768]{2,1,0:T(8,128)S(1)}, f32[2,512,768]{2,1,0:T(8,128)}, u32[]{:S(2)}) copy-start(f32[2,512,768]{2,1,0:T(8,128)} %copy-done.2) | copy-start | bytes 9437188
  364.8 1.4 copy-start.14
  366.0 2.8 copy-start.10
  366.0 2.8 copy-start.47
  368.7 228.8 %reduce-scatter.8.cloned.1.call-start = ((), (), s32[]{:S(2)}) async-start(), calls=%async_computation.11 | async-start | bytes 3981312 | tf_op jit(solution)/shard_map/reduce_scatter | solution.py:308
  375.2 6.4 copy-start.9
  384.0 11.6 %slice-start = ((s8[12582912]{0:T(1024)(128)(4,1)}), s8[4194304]{0:T(1024)(128)(4,1)S(1)}, s32[]{:S(2)}) async-start(s8[12582912]{0:T(1024)(128)(4,1)} %bitcast.162), calls=%async_computation.16 | async-start | bytes 8388608 | tf_op jit(solution)/shard_map/while
  384.0 11.5 %slice-start.1 = ((s8[12582912]{0:T(1024)(128)(4,1)}), s8[4194304]{0:T(1024)(128)(4,1)S(1)}, s32[]{:S(2)}) async-start(s8[12582912]{0:T(1024)(128)(4,1)} %bitcast.162), calls=%async_computation.17 | async-start | bytes 8388608 | tf_op jit(solution)/shard_map/while
  384.0 12.8 %slice-start.2 = ((s8[12582912]{0:T(1024)(128)(4,1)}), s8[4194304]{0:T(1024)(128)(4,1)S(1)}, s32[]{:S(2)}) async-start(s8[12582912]{0:T(1024)(128)(4,1)} %bitcast.162), calls=%async_computation.18 | async-start | bytes 8388608 | tf_op jit(solution)/shard_map/while
  413.7 6.4 copy-start.9
  422.5 11.5 %slice-start = ((s8[12582912]{0:T(1024)(128)(4,1)}), s8[4194304]{0:T(1024)(128)(4,1)S(1)}, s32[]{:S(2)}) async-start(s8[12582912]{0:T(1024)(128)(4,1)} %bitcast.162), calls=%async_computation.16 | async-start | bytes 8388608 | tf_op jit(solution)/shard_map/while
  422.5 11.5 %slice-start.1 = ((s8[12582912]{0:T(1024)(128)(4,1)}), s8[4194304]{0:T(1024)(128)(4,1)S(1)}, s32[]{:S(2)}) async-start(s8[12582912]{0:T(1024)(128)(4,1)} %bitcast.162), calls=%async_computation.17 | async-start | bytes 8388608 | tf_op jit(solution)/shard_map/while
  422.6 12.7 %slice-start.2 = ((s8[12582912]{0:T(1024)(128)(4,1)}), s8[4194304]{0:T(1024)(128)(4,1)S(1)}, s32[]{:S(2)}) async-start(s8[12582912]{0:T(1024)(128)(4,1)} %bitcast.162), calls=%async_computation.18 | async-start | bytes 8388608 | tf_op jit(solution)/shard_map/while
  459.8 1.9 copy-start.1
  459.8 1.9 copy-start.25
  459.8 1.9 copy-start.27
  459.8 1.9 copy-start.36
  459.8 1.9 copy-start.43
  459.8 1.9 copy-start.50
  459.8 176.7 %reduce-scatter.14.cloned.1.call-start = ((), (), s32[]{:S(2)}) async-start(), calls=%async_computation.14 | async-start | bytes 5308416 | tf_op jit(solution)/shard_map/reduce_scatter | solution.py:323
  472.9 262.4 %reduce-scatter.12.cloned.1.call-start = ((), (), s32[]{:S(2)}) async-start(), calls=%async_computation.13 | async-start | bytes 5308416 | tf_op jit(solution)/shard_map/reduce_scatter | solution.py:320
  484.3 9.2 %copy-start.23 = (f32[768]{0:T(1024)S(1)}, f32[768]{0:T(1024)}, u32[]{:S(2)}) copy-start(f32[768]{0:T(1024)} %copy-done.22) | copy-start | bytes 9220
  484.3 9.2 %copy-start.29 = (s32[2,512]{1,0:T(2,128)S(1)}, s32[2,512]{1,0:T(2,128)}, u32[]{:S(2)}) copy-start(s32[2,512]{1,0:T(2,128)} %param.33) | copy-start | bytes 12292
  484.3 318.7 %reduce-scatter.6.cloned.1.call-start = ((), (), s32[]{:S(2)}) async-start(), calls=%async_computation.10 | async-start | bytes 1327104 | tf_op jit(solution)/shard_map/reduce_scatter | solution.py:305
  484.9 8.6 copy-start.5
  484.9 8.6 copy-start.31
  493.6 3.0 copy-start.7
  493.6 46.7 %copy-start.16 = (bf16[2,128,768]{2,1,0:T(8,128)(2,1)S(1)}, bf16[2,128,768]{2,1,0:T(8,128)(2,1)}, u32[]{:S(2)}) copy-start(bf16[2,128,768]{2,1,0:T(8,128)(2,1)} %copy-done.15) | copy-start | bytes 1179652
  540.2 55.1 %copy-start.37 = (f32[2,512]{1,0:T(2,128)S(1)}, f32[2,512]{1,0:T(2,128)}, u32[]{:S(2)}) copy-start(f32[2,512]{1,0:T(2,128)} %copy-done.35) | copy-start | bytes 12292
  541.8 309.4 %all-reduce.18.cloned.1.call-start = ((), (), s32[]{:S(2)}) async-start(), calls=%async_computation.15 | async-start | bytes 3538944 | tf_op jit(solution)/shard_map/psum | solution.py:337
  595.4 140.0 %copy-start.18 = (bf16[2,128,768]{2,1,0:T(8,128)(2,1)S(1)}, bf16[2,128,768]{2,1,0:T(8,128)(2,1)}, u32[]{:S(2)}) copy-start(bf16[2,128,768]{2,1,0:T(8,128)(2,1)} %copy-done.17) | copy-start | bytes 1179652
  597.6 139.6 %copy-start.8 = (f32[2,512,768]{2,1,0:T(8,128)S(1)}, f32[2,512,768]{2,1,0:T(8,128)}, u32[]{:S(2)}) copy-start(f32[2,512,768]{2,1,0:T(8,128)} %copy-done.7) | copy-start | bytes 9437188
  851.2 4.4 copy-start.19
  851.2 5.4 copy-start.20
  (6 other events, 4.2 us)
Sparse Core Ops, SparseCore 0:
  10.2 44.0 all-gather.6
  56.5 64.8 all-gather.8
  123.5 39.6 all-gather.10
  165.3 78.6 all-gather.12
  246.0 78.0 all-gather.14
  368.9 62.1 reduce-scatter.9
  460.0 77.3 reduce-scatter.7
  541.0 95.5 reduce-scatter.13
  640.2 95.1 reduce-scatter.11
  739.1 63.7 reduce-scatter.5
  805.6 45.5 all-reduce.17
